TPU v7x, 512 devices: a whole 4x8x8 slice. The times are simulated.
512 devices in a mesh: row: 32 (over x_lo, y, core), col: 16 (over z, x_hi).
Axes of the slice: x: 4 (x_hi: 2, x_lo: 2; x = x_hi * 2 + x_lo), y: 8, z: 8, core: 2. Of those that a mesh axis runs over, the one named last changes fastest.
Arguments:
- x_slab: float32 [8192, 4096], P('col', 'row'), may hold values from -5400 to 5400, as said below
- weight_c: float32 [1], replicated, may hold values from 2048 to 16384
Outputs:
- trailing: float32 [4096, 4096], P('row', 'col')
- panels: float32 [4096, 512], P('row')
- inverses: float32 [2, 256, 256], replicated
- frobenius: float32 [1], replicated
Inputs may be any that keep to these rules, and one draw needn't show every extreme that they name: `x_slab`: real-valued entries.
All inputs are finite; a program needn't handle non-finite values.
Results may differ from a plain program's by a relative error of at most 0.00015.
Values sent between devices are 32-bit elements; how exact they have to be, the bound alone decides.
A program may use at most 64 MiB of HBM per device.

v0:
```python
import jax
import jax.numpy as jnp
from jax import lax
from jax.sharding import Mesh
from jax.sharding import PartitionSpec as P

PANEL = 256
COL = ("col_0", "col_1")
ROW = ("row_0", "row_1", "row_2")
ROW_COL = ("row_0", "row_1", "row_2", "col_0", "col_1")
HIGH = lax.Precision.HIGHEST


def broadcast(x, axis, root):
    return lax.dynamic_index_in_dim(lax.all_gather(x, axis), root, 0, keepdims=False)


def split_up(x, dim, size):
    dims = x.shape
    blocks = x.reshape(*dims[:dim], size, dims[dim] // size, *dims[dim + 1 :])
    return jnp.moveaxis(blocks, dim, 0)


def summed_on_arrival(x, axis, dim):
    blocks = split_up(x, dim, lax.axis_size(axis))
    arrived = lax.all_to_all(blocks, axis, split_axis=0, concat_axis=0, tiled=True)
    return arrived.sum(axis=0)


def rows_for(lines, size):
    spare = -len(lines) % size
    return jnp.pad(lines, [(0, spare)] + [(0, 0)] * (lines.ndim - 1))


def joined_along(blocks, dim):
    blocks = jnp.moveaxis(blocks, 0, dim)
    dims = blocks.shape
    return blocks.reshape(*dims[:dim], dims[dim] * dims[dim + 1], *dims[dim + 2 :])


def from_everyone(x, axis):
    size = lax.axis_size(axis)
    return lax.all_to_all(jnp.broadcast_to(x[None], (size, *x.shape)), axis, 0, 0, tiled=True)


def collect(x, axis, dim):
    return joined_along(from_everyone(x, axis), dim)


def sum_by_parts(x, axes):
    lines = x.reshape(-1, x.shape[-1])
    own = summed_on_arrival(rows_for(lines, lax.axis_size(axes)), axes, 0)
    whole = collect(own, axes, 0)
    return whole[: len(lines)].reshape(x.shape)


def by_axis(x, axes):
    for axis in axes:
        x = lax.psum(x, axis)
    return x


def nested_sum(x, axes):
    own = summed_on_arrival(rows_for(x, lax.axis_size(axes)), axes, 0)
    whole = collect(own, axes, 0)
    return whole[: len(x)].reshape(x.shape)


def packed_total(arrays, axis):
    ends = [0]
    for a in arrays:
        ends.append(ends[-1] + a.size)
    subtotal = nested_sum(jnp.concatenate([a.ravel() for a in arrays]), axis)
    return tuple((subtotal[b:e].reshape(a.shape) for a, b, e in zip(arrays, ends, ends[1:])))


def product(left, right):
    return jnp.dot(left, right, preferred_element_type=jnp.float32, precision=HIGH)


def invert_lower(block):
    factor = jnp.linalg.cholesky(block)
    identity = jnp.eye(block.shape[0], dtype=block.dtype)
    return lax.linalg.triangular_solve(factor, identity, left_side=True, lower=True)


def lower_panel(column, inverse, start, row_ids, panel_size):
    values = product(column, inverse.T)
    targets = start + jnp.arange(panel_size, dtype=jnp.int32)
    return jnp.where(row_ids[:, None] >= targets[None, :], values, jnp.zeros_like(values))


def panel_column(matrix, number, panel_size, tile_cols):
    owner = number * panel_size // tile_cols
    return broadcast(matrix, COL, owner)


def pick_rows(values, start, row_ids, panel_size):
    targets = start + jnp.arange(panel_size, dtype=jnp.int32)
    selector = (targets[:, None] == row_ids[None, :]).astype(jnp.float32)
    return product(selector, values)


def diagonal_block(column, start, row_ids, panel_size):
    return sum_by_parts(pick_rows(column, start, row_ids, panel_size), ROW)


def on_device(x_slab, weight_c):
    local_cols = x_slab.shape[1]
    width = local_cols * lax.axis_size(ROW)
    tile_cols = width // lax.axis_size(COL)
    panel_size = PANEL
    row_ids = lax.axis_index(ROW) * local_cols + jnp.arange(local_cols, dtype=jnp.int32)
    col_ids = lax.axis_index(COL) * tile_cols + jnp.arange(tile_cols, dtype=jnp.int32)
    squares = by_axis(jnp.sum(x_slab * x_slab), ROW_COL)
    factor_c = weight_c[0] / squares
    partial_value = lax.dot_general(
        x_slab,
        lax.all_gather(x_slab, ROW, axis=1, tiled=True),
        (((0,), (0,)), ((), ())),
        precision=HIGH,
        preferred_element_type=jnp.float32,
    )
    block = summed_on_arrival(partial_value, COL, 1)
    gram = block * factor_c + (row_ids[:, None] == col_ids[None, :]).astype(jnp.float32)
    column_one = panel_column(gram, 0, panel_size, tile_cols)
    column_two = panel_column(gram, 1, panel_size, tile_cols)
    inverse_one = invert_lower(diagonal_block(column_one, 0, row_ids, panel_size))
    lower_one = lower_panel(column_one, inverse_one, 0, row_ids, panel_size)
    raw_block, crossing = packed_total(
        (
            pick_rows(column_two, panel_size, row_ids, panel_size),
            pick_rows(lower_one, panel_size, row_ids, panel_size),
        ),
        ROW,
    )
    inverse_two = invert_lower(raw_block - product(crossing, crossing.T))
    lower_two = lower_panel(
        column_two - product(lower_one, crossing.T), inverse_two, panel_size, row_ids, panel_size
    )
    both = jnp.concatenate([lower_one, lower_two], axis=1)
    gathered = lax.all_gather(both, ROW, axis=0, tiled=True)
    mine = lax.dynamic_slice_in_dim(gathered, lax.axis_index(COL) * tile_cols, tile_cols, 0)
    matrix = gram - product(both, mine.T)
    inverses = [inverse_one, inverse_two]
    return (matrix, both, jnp.stack(inverses), jnp.sqrt(squares).reshape(1))


def solution(mesh):
    split = Mesh(mesh.devices.reshape(2, 8, 2, 8, 2), ("row_0", "row_1", "row_2", "col_0", "col_1"))
    in_specs = (P(COL, ROW), P())
    out_specs = (P(ROW, COL), P(ROW, None), P(), P())
    return jax.shard_map(
        on_device, mesh=split, in_specs=in_specs, out_specs=out_specs, check_vma=False
    )
```

profile of v0, /device:TPU:1, one launch (start us, length us, event | category | flops | bytes accessed | tf_op | source)
XLA Modules:
  0.0 585.1 jit_solution(13100792732569455945)
XLA Ops:
  7.2 0.7 all-gather.4.cloned.1.call-update
  7.9 98.4 %all-gather.4.cloned.1.call-done = f32[512,4096]{1,0:T(8,128)} async-done(((f32[512,128]{1,0:T(8,128)}), f32[512,4096]{1,0:T(8,128)}) %all-gather.4.cloned.1.call-update) | async-done | bytes 8388624 | tf_op jit(solution)/shard_map/all_gather | solution.py:119
  106.3 6.9 %fusion.41 = f32[128,4096]{1,0:T(8,128)S(1)} fusion(f32[512,128]{1,0:T(8,128)} %param.5, f32[512,4096]{1,0:T(8,128)} %all-gather.4.cloned.1.call-done), kind=kOutput, calls=%fused_computation.97 | convolution fusion | flops 3221225472 | bytes 10747904 | tf_op jit(solution)/shard_map/dot_general | solution.py:117
  113.2 1.6 copy.21
  114.8 9.5 %all-to-all-start = ((f32[16,128,256]{2,1,0:T(8,128)}), f32[16,128,256]{2,1,0:T(8,128)S(1)}, u32[]{:S(2)}, u32[]{:S(2)}) async-start(f32[16,128,256]{2,1,0:T(8,128)} %bitcast.100), calls=%async_computation | async-start | bytes 4194304 | tf_op jit(solution)/shard_map/all_to_all | solution.py:26
  124.4 0.7 multiply_reduce_fusion
  125.0 4.4 psum.35
  129.4 15.1 %psum.36 = f32[]{:T(128)} all-reduce(f32[]{:T(128)} %psum.35), channel_id=1, replica_groups=mesh['row_0'=2,'row_1'=8,'row_2'=2,'col_0'=8,'col_1'=2] {'row_1'}, use_global_device_ids=true, to_apply=%region_3.0 | all-reduce | flops 1 | bytes 8 | tf_op jit(solution)/shard_map/psum | solution.py:59
  144.5 6.4 %psum.37 = f32[]{:T(128)} all-reduce(f32[]{:T(128)} %psum.36), channel_id=1, replica_groups=mesh['row_0'=2,'row_1'=8,'row_2'=2,'col_0'=8,'col_1'=2] {'row_2'}, use_global_device_ids=true, to_apply=%region_4.0 | all-reduce | flops 1 | bytes 8 | tf_op jit(solution)/shard_map/psum | solution.py:59
  151.0 28.8 %psum.38 = f32[]{:T(128)} all-reduce(f32[]{:T(128)} %psum.37), channel_id=1, replica_groups=mesh['row_0'=2,'row_1'=8,'row_2'=2,'col_0'=8,'col_1'=2] {'col_0'}, use_global_device_ids=true, to_apply=%region_5.0 | all-reduce | flops 1 | bytes 8 | tf_op jit(solution)/shard_map/psum | solution.py:59
  179.8 5.9 %psum.39 = f32[]{:T(128)} all-reduce(f32[]{:T(128)} %psum.38), channel_id=1, replica_groups=mesh['row_0'=2,'row_1'=8,'row_2'=2,'col_0'=8,'col_1'=2] {'col_1'}, use_global_device_ids=true, to_apply=%region_6.0 | all-reduce | flops 1 | bytes 8 | tf_op jit(solution)/shard_map/psum | solution.py:59
  187.1 0.7 bitcast_add_fusion.2
  187.9 90.3 %all-gather.6.cloned.1.call-done = f32[16,128,256]{2,1,0:T(8,128)} async-done(((f32[1,128,256]{2,1,0:T(8,128)}), f32[16,128,256]{2,1,0:T(8,128)}) %all-gather.6.cloned.1.call-update) | async-done | bytes 2097168 | tf_op jit(solution)/shard_map/all_gather | solution.py:15
  278.2 1.2 fusion.10
  279.4 22.4 %all_to_all.30 = f32[32,8,256]{2,1,0:T(8,128)S(1)} all-to-all(f32[32,8,256]{2,1,0:T(8,128)S(1)} %fusion.10), channel_id=1, replica_groups=mesh['row_0'=2,'row_1'=8,'row_2'=2,'col_0'=8,'col_1'=2] {'row_0','row_1'..., dimensions={0} | all-to-all | bytes 524288 | tf_op jit(solution)/shard_map/all_to_all | solution.py:26
  301.8 0.7 broadcast_in_dim.4
  302.5 5.8 all-to-all-start.2
  308.4 1.2 fusion.8
  309.7 10.4 %all-to-all-done.2 = f32[32,8,256]{2,1,0:T(8,128)S(1)} async-done(((f32[32,8,256]{2,1,0:T(8,128)}), f32[32,8,256]{2,1,0:T(8,128)S(1)}, u32[]{:S(2)}, u32[]{:S(2)}) %all-to-all-start.2) | async-done | bytes 262176 | tf_op jit(solution)/shard_map/all_to_all | solution.py:43
  320.3 11.7 %cholesky.130 = f32[128,128]{1,0:T(8,128)S(1)} custom-call(f32[128,128]{1,0:T(8,128)S(1)} %cholesky.194), custom_call_target="Cholesky" | custom-call | tf_op jit(solution)/shard_map/jit(cholesky)/cholesky | solution.py:82
  332.1 9.8 %custom-call.13 = f32[1,128,128]{1,2,0:T(8,128)S(1)} custom-call(f32[1,128,128]{2,1,0:T(8,128)S(1)} %get-tuple-element.51), custom_call_target="InvertDiagBlocksLowerTriangular" | custom-call | tf_op jit(solution)/shard_map/jit(cholesky)/cholesky | solution.py:82
  342.1 0.3 convolution_subtract_fusion.6
  342.4 11.7 %cholesky.147 = f32[128,128]{1,0:T(8,128)S(1)} custom-call(f32[128,128]{1,0:T(8,128)S(1)} %convolution_subtract_fusion.6), custom_call_target="Cholesky" | custom-call | tf_op jit(solution)/shard_map/jit(cholesky)/cholesky | solution.py:82
  354.2 0.6 compare_reduce_fusion.2
  356.2 4.0 while.4
  356.3 0.6 fusion.61
  356.8 1.4 bitcast_dynamic-update-slice_fusion.4
  358.3 0.6 fusion.61
  358.8 1.4 bitcast_dynamic-update-slice_fusion.4
  360.2 31.8 %custom-call.14 = f32[2,128,128]{1,2,0:T(8,128)S(1)} custom-call(f32[2,128,128]{2,1,0:T(8,128)S(1)} %get-tuple-element.20), custom_call_target="InvertDiagBlocksLowerTriangular" | custom-call | tf_op jit(solution)/shard_map/triangular_solve/custom-call.0 | solution.py:84
  392.1 0.3 fusion.16
  392.4 0.3 convolution_subtract_fusion.4
  392.6 0.3 fusion.25
  393.0 1.3 convolution_select_fusion.1
  394.3 0.3 fusion.6
  394.7 0.6 all_to_all.22
  395.3 21.0 %all_to_all.31 = f32[32,1,4096]{2,1,0:T(1,128)S(1)} all-to-all(f32[32,1,4096]{2,1,0:T(1,128)S(1)} %all_to_all.22), channel_id=1, replica_groups=mesh['row_0'=2,'row_1'=8,'row_2'=2,'col_0'=8,'col_1'=2] {'row_0','row_1'..., dimensions={0} | all-to-all | bytes 1048576 | tf_op jit(solution)/shard_map/all_to_all | solution.py:26
  416.2 0.4 reduce_sum.39
  416.6 1.3 broadcast_in_dim.5
  417.8 5.6 all-to-all-start.4
  423.5 16.7 %all-to-all-done.4 = f32[32,1,4096]{2,1,0:T(1,128)S(1)} async-done(((f32[32,1,4096]{2,1,0:T(1,128)}), f32[32,1,4096]{2,1,0:T(1,128)S(1)}, u32[]{:S(2)}, u32[]{:S(2)}) %all-to-all-start.4) | async-done | bytes 524320 | tf_op jit(solution)/shard_map/all_to_all | solution.py:43
  440.2 1.3 slice_reduce_fusion
  441.7 0.4 convolution_subtract_fusion
  442.4 11.7 %cholesky.164 = f32[128,128]{1,0:T(8,128)S(1)} custom-call(f32[128,128]{1,0:T(8,128)S(1)} %cholesky.197), custom_call_target="Cholesky" | custom-call | tf_op jit(solution)/shard_map/jit(cholesky)/cholesky | solution.py:82
  454.1 9.8 %custom-call.15 = f32[1,128,128]{1,2,0:T(8,128)S(1)} custom-call(f32[1,128,128]{2,1,0:T(8,128)S(1)} %get-tuple-element.47), custom_call_target="InvertDiagBlocksLowerTriangular" | custom-call | tf_op jit(solution)/shard_map/jit(cholesky)/cholesky | solution.py:82
  464.2 0.3 convolution_subtract_fusion.5
  464.4 11.8 %cholesky.181 = f32[128,128]{1,0:T(8,128)S(1)} custom-call(f32[128,128]{1,0:T(8,128)S(1)} %convolution_subtract_fusion.5), custom_call_target="Cholesky" | custom-call | tf_op jit(solution)/shard_map/jit(cholesky)/cholesky | solution.py:82
  476.3 0.6 compare_reduce_fusion
  476.9 0.6 compare_reduce_fusion.1
  478.9 4.0 while.5
  478.9 0.6 fusion.62
  479.5 1.4 bitcast_dynamic-update-slice_fusion.5
  480.9 0.6 fusion.62
  481.5 1.4 bitcast_dynamic-update-slice_fusion.5
  482.9 19.7 %custom-call.16 = f32[2,128,128]{1,2,0:T(8,128)S(1)} custom-call(f32[2,128,128]{2,1,0:T(8,128)S(1)} %get-tuple-element.21), custom_call_target="InvertDiagBlocksLowerTriangular" | custom-call | tf_op jit(solution)/shard_map/triangular_solve/custom-call.0 | solution.py:84
  502.6 0.3 fusion.14
  502.9 0.3 convolution_subtract_fusion.3
  503.2 0.3 fusion.21
  503.5 1.3 convolution_subtract_fusion.2
  504.8 0.4 convolution_select_fusion
  505.2 0.7 pad_maximum_fusion.4
  506.7 0.8 pad_maximum_fusion.1
  507.5 67.3 %all-gather.8.cloned.1.call-done = f32[4096,512]{1,0:T(8,128)} async-done(((f32[128,512]{1,0:T(8,128)}), f32[4096,512]{1,0:T(8,128)}) %all-gather.8.cloned.1.call-update) | async-done | bytes 8388624 | tf_op jit(solution)/shard_map/all_gather | solution.py:142
  574.8 2.4 convolution_subtract_fusion.1
  (49 shorter events, 1.9 us)
Async XLA Ops:
  7.2 99.1 %all-gather.4.cloned.1.call-start = ((), (), s32[]{:S(2)}) async-start(), calls=%async_computation.5 | async-start | bytes 8650752 | tf_op jit(solution)/shard_map/all_gather | solution.py:119
  114.8 9.6 %copy-start.1 = (f32[512,128]{1,0:T(8,128)S(1)}, f32[512,128]{1,0:T(8,128)}, u32[]{:S(2)}) copy-start(f32[512,128]{1,0:T(8,128)} %param.5) | copy-start | bytes 786436
  114.8 72.2 %all-to-all-start = ((f32[16,128,256]{2,1,0:T(8,128)}), f32[16,128,256]{2,1,0:T(8,128)S(1)}, u32[]{:S(2)}, u32[]{:S(2)}) async-start(f32[16,128,256]{2,1,0:T(8,128)} %bitcast.100), calls=%async_computation | async-start | bytes 4194304 | tf_op jit(solution)/shard_map/all_to_all | solution.py:26
  124.3 153.9 %all-gather.6.cloned.1.call-start = ((), (), s32[]{:S(2)}) async-start(), calls=%async_computation.6 | async-start | bytes 2228224 | tf_op jit(solution)/shard_map/all_gather | solution.py:15
  302.5 17.6 %all-to-all-start.2 = ((f32[32,8,256]{2,1,0:T(8,128)}), f32[32,8,256]{2,1,0:T(8,128)S(1)}, u32[]{:S(2)}, u32[]{:S(2)}) async-start(f32[32,8,256]{2,1,0:T(8,128)} %broadcast_in_dim.4), calls=%async_computation.2 | async-start | bytes 524288 | tf_op jit(solution)/shard_map/all_to_all | solution.py:43
  417.8 22.3 %all-to-all-start.4 = ((f32[32,1,4096]{2,1,0:T(1,128)}), f32[32,1,4096]{2,1,0:T(1,128)S(1)}, u32[]{:S(2)}, u32[]{:S(2)}) async-start(f32[32,1,4096]{2,1,0:T(1,128)} %broadcast_in_dim.5), calls=%async_computation.4 | async-start | bytes 1048576 | tf_op jit(solution)/shard_map/all_to_all | solution.py:43
  423.5 151.4 %all-gather.8.cloned.1.call-start = ((), (), s32[]{:S(2)}) async-start(), calls=%async_computation.7 | async-start | bytes 8650752 | tf_op jit(solution)/shard_map/all_gather | solution.py:142
  506.0 68.9 %copy-start = (f32[128,512]{1,0:T(8,128)S(1)}, f32[128,512]{1,0:T(8,128)}, u32[]{:S(2)}) copy-start(f32[128,512]{1,0:T(8,128)} %pad_maximum_fusion.4) | copy-start | bytes 786436
Sparse Core Ops, SparseCore 0:
  10.0 96.2 all-gather.3
  188.0 90.1 all-gather.5
  506.1 68.6 all-gather.7
where the time goes:
time: 590 us; the launch traced here: 585 us
  waiting for transfers between devices  284 us (48%)
  other arithmetic  124 us (21%)
  blocking collectives  104 us (18%)
  starting transfers between devices  21.1 us (4%)
  between operations  20.1 us (3%)
  matrix products  18.1 us (3%)
  local copies, waits for them, and re-layouts  14.1 us (2%)
    all_gather x1, waiting for transfers between devices, on_device(): lax.all_gather(x_slab, ROW, axis=1, tiled=True)  98.4 us
    all_gather x1, waiting for transfers between devices, broadcast(): lax.all_gather(x, axis)  90.3 us
    another operation x13, other arithmetic, invert_lower(): factor = jnp.linalg.cholesky(block)  68.6 us
    all_gather x1, waiting for transfers between devices, on_device(): gathered = lax.all_gather(both, ROW, axis=0, tiled=True)  67.3 us
    psum x5, blocking collectives, by_axis(): x = lax.psum(x, axis)  60.7 us
    another operation x5, other arithmetic, invert_lower(): lax.linalg.triangular_solve(factor, identity, left_side=True, lower=True)  51.5 us
    all_to_all x2, blocking collectives, summed_on_arrival(): lax.all_to_all(blocks, axis, split_axis=0, concat_axis=0, tiled=True)  43.3 us
    all_to_all x2, waiting for transfers between devices, from_everyone(): lax.all_to_all(jnp.broadcast_to(x[None], (size, *x.shape)), axis, 0, 0, t...  27.1 us
  transfers between devices with their start and end apart: 6, of which 5 were waited for; matrix products, arithmetic and copies ran while one was open for 0% of the time, Pallas kernels for 0%

commit v1 on v0

--- a/solution.py
+++ b/solution.py
@@ -139,7 +139,9 @@
         column_two - product(lower_one, crossing.T), inverse_two, panel_size, row_ids, panel_size
     )
     both = jnp.concatenate([lower_one, lower_two], axis=1)
-    gathered = lax.all_gather(both, ROW, axis=0, tiled=True)
+    gathered = jnp.concatenate(
+        lax.all_to_all(jnp.stack([both] * lax.axis_size(ROW)), ROW, 0, 0), axis=0
+    )
     mine = lax.dynamic_slice_in_dim(gathered, lax.axis_index(COL) * tile_cols, tile_cols, 0)
     matrix = gram - product(both, mine.T)
     inverses = [inverse_one, inverse_two]

time: 590 us -> 718 us (1.22)
  waiting for transfers between devices: 284 us -> 399 us
    all_to_all x0 -> x1, waiting for transfers between devices: none -> 183 us  [on_device(): lax.all_to_all(jnp.stack([both] * lax.axis_size(ROW)), ROW, 0, 0)]
    all_gather x1 -> x0, waiting for transfers between devices: 67.3 us -> none  [on_device(): gathered = lax.all_gather(both, ROW, axis=0, tiled=True)]
where the time goes in v1:
time: 718 us; the launch traced here: 711 us
  waiting for transfers between devices  399 us (56%)
  other arithmetic  123 us (17%)
  blocking collectives  104 us (14%)
  starting transfers between devices  27.6 us (4%)
  between operations  20.3 us (3%)
  local copies, waits for them, and re-layouts  18.4 us (3%)
  matrix products  18.1 us (3%)
    all_to_all x1, waiting for transfers between devices, on_device(): lax.all_to_all(jnp.stack([both] * lax.axis_size(ROW)), ROW, 0, 0)  183 us
    all_gather x1, waiting for transfers between devices, on_device(): lax.all_gather(x_slab, ROW, axis=1, tiled=True)  98.4 us
    all_gather x1, waiting for transfers between devices, broadcast(): lax.all_gather(x, axis)  90.3 us
    another operation x13, other arithmetic, invert_lower(): factor = jnp.linalg.cholesky(block)  68.6 us
    psum x5, blocking collectives, by_axis(): x = lax.psum(x, axis)  60.7 us
    another operation x5, other arithmetic, invert_lower(): lax.linalg.triangular_solve(factor, identity, left_side=True, lower=True)  51.5 us
    all_to_all x2, blocking collectives, summed_on_arrival(): lax.all_to_all(blocks, axis, split_axis=0, concat_axis=0, tiled=True)  43.3 us
    all_to_all x2, waiting for transfers between devices, from_everyone(): lax.all_to_all(jnp.broadcast_to(x[None], (size, *x.shape)), axis, 0, 0, t...  27.2 us
  transfers between devices with their start and end apart: 6, of which 5 were waited for; matrix products, arithmetic and copies ran while one was open for 0% of the time, Pallas kernels for 0%

profile of v1, /device:TPU:1, one launch (start us, length us, event | category | flops | bytes accessed | tf_op | source)
XLA Modules:
  0.0 710.9 jit_solution(11933141065230400715)
XLA Ops:
  7.2 0.7 all-gather.3.cloned.1.call-update
  7.9 98.4 %all-gather.3.cloned.1.call-done = f32[512,4096]{1,0:T(8,128)} async-done(((f32[512,128]{1,0:T(8,128)}), f32[512,4096]{1,0:T(8,128)}) %all-gather.3.cloned.1.call-update) | async-done | bytes 8388624 | tf_op jit(solution)/shard_map/all_gather | solution.py:119
  106.3 6.9 fusion.41
  113.2 1.6 copy.21
  114.8 9.5 %all-to-all-start = ((f32[16,128,256]{2,1,0:T(8,128)}), f32[16,128,256]{2,1,0:T(8,128)S(1)}, u32[]{:S(2)}, u32[]{:S(2)}) async-start(f32[16,128,256]{2,1,0:T(8,128)} %bitcast.101), calls=%async_computation | async-start | bytes 4194304 | tf_op jit(solution)/shard_map/all_to_all | solution.py:26
  124.4 0.7 multiply_reduce_fusion
  125.0 4.4 psum.35
  129.4 15.1 %psum.36 = f32[]{:T(128)} all-reduce(f32[]{:T(128)} %psum.35), channel_id=1, replica_groups=mesh['row_0'=2,'row_1'=8,'row_2'=2,'col_0'=8,'col_1'=2] {'row_1'}, use_global_device_ids=true, to_apply=%region_3.0 | all-reduce | flops 1 | bytes 8 | tf_op jit(solution)/shard_map/psum | solution.py:59
  144.5 6.4 psum.37
  151.0 28.8 %psum.38 = f32[]{:T(128)} all-reduce(f32[]{:T(128)} %psum.37), channel_id=1, replica_groups=mesh['row_0'=2,'row_1'=8,'row_2'=2,'col_0'=8,'col_1'=2] {'col_0'}, use_global_device_ids=true, to_apply=%region_5.0 | all-reduce | flops 1 | bytes 8 | tf_op jit(solution)/shard_map/psum | solution.py:59
  179.8 5.9 psum.39
  187.1 0.7 bitcast_add_fusion.2
  187.9 90.3 %all-gather.5.cloned.1.call-done = f32[16,128,256]{2,1,0:T(8,128)} async-done(((f32[1,128,256]{2,1,0:T(8,128)}), f32[16,128,256]{2,1,0:T(8,128)}) %all-gather.5.cloned.1.call-update) | async-done | bytes 2097168 | tf_op jit(solution)/shard_map/all_gather | solution.py:15
  278.2 1.2 fusion.10
  279.4 22.4 %all_to_all.35 = f32[32,8,256]{2,1,0:T(8,128)S(1)} all-to-all(f32[32,8,256]{2,1,0:T(8,128)S(1)} %fusion.10), channel_id=1, replica_groups=mesh['row_0'=2,'row_1'=8,'row_2'=2,'col_0'=8,'col_1'=2] {'row_0','row_1'..., dimensions={0} | all-to-all | bytes 524288 | tf_op jit(solution)/shard_map/all_to_all | solution.py:26
  301.8 0.7 broadcast_in_dim.4
  302.5 5.8 all-to-all-start.2
  308.4 1.2 fusion.8
  309.7 10.4 %all-to-all-done.2 = f32[32,8,256]{2,1,0:T(8,128)S(1)} async-done(((f32[32,8,256]{2,1,0:T(8,128)}), f32[32,8,256]{2,1,0:T(8,128)S(1)}, u32[]{:S(2)}, u32[]{:S(2)}) %all-to-all-start.2) | async-done | bytes 262176 | tf_op jit(solution)/shard_map/all_to_all | solution.py:43
  320.4 11.7 %cholesky.130 = f32[128,128]{1,0:T(8,128)S(1)} custom-call(f32[128,128]{1,0:T(8,128)S(1)} %cholesky.194), custom_call_target="Cholesky" | custom-call | tf_op jit(solution)/shard_map/jit(cholesky)/cholesky | solution.py:82
  332.1 9.8 %custom-call.13 = f32[1,128,128]{1,2,0:T(8,128)S(1)} custom-call(f32[1,128,128]{2,1,0:T(8,128)S(1)} %get-tuple-element.51), custom_call_target="InvertDiagBlocksLowerTriangular" | custom-call | tf_op jit(solution)/shard_map/jit(cholesky)/cholesky | solution.py:82
  342.2 0.3 convolution_subtract_fusion.6
  342.4 11.7 %cholesky.147 = f32[128,128]{1,0:T(8,128)S(1)} custom-call(f32[128,128]{1,0:T(8,128)S(1)} %convolution_subtract_fusion.6), custom_call_target="Cholesky" | custom-call | tf_op jit(solution)/shard_map/jit(cholesky)/cholesky | solution.py:82
  354.2 0.6 compare_reduce_fusion.2
  356.2 4.0 while.4
  356.3 0.6 fusion.61
  356.9 1.4 bitcast_dynamic-update-slice_fusion.4
  358.3 0.6 fusion.61
  358.9 1.4 bitcast_dynamic-update-slice_fusion.4
  360.3 31.8 %custom-call.14 = f32[2,128,128]{1,2,0:T(8,128)S(1)} custom-call(f32[2,128,128]{2,1,0:T(8,128)S(1)} %get-tuple-element.20), custom_call_target="InvertDiagBlocksLowerTriangular" | custom-call | tf_op jit(solution)/shard_map/triangular_solve/custom-call.0 | solution.py:84
  392.1 0.3 fusion.16
  392.6 0.3 fusion.25
  393.0 1.3 convolution_select_fusion.1
  394.3 0.3 fusion.6
  394.7 0.6 all_to_all.25
  395.3 21.0 %all_to_all.36 = f32[32,1,4096]{2,1,0:T(1,128)S(1)} all-to-all(f32[32,1,4096]{2,1,0:T(1,128)S(1)} %all_to_all.25), channel_id=1, replica_groups=mesh['row_0'=2,'row_1'=8,'row_2'=2,'col_0'=8,'col_1'=2] {'row_0','row_1'..., dimensions={0} | all-to-all | bytes 1048576 | tf_op jit(solution)/shard_map/all_to_all | solution.py:26
  416.2 0.4 reduce_sum.39
  416.6 1.3 broadcast_in_dim.5
  417.9 5.6 all-to-all-start.4
  423.5 16.7 %all-to-all-done.4 = f32[32,1,4096]{2,1,0:T(1,128)S(1)} async-done(((f32[32,1,4096]{2,1,0:T(1,128)}), f32[32,1,4096]{2,1,0:T(1,128)S(1)}, u32[]{:S(2)}, u32[]{:S(2)}) %all-to-all-start.4) | async-done | bytes 524320 | tf_op jit(solution)/shard_map/all_to_all | solution.py:43
  440.2 1.3 slice_reduce_fusion
  441.8 0.4 convolution_subtract_fusion
  442.4 11.7 %cholesky.164 = f32[128,128]{1,0:T(8,128)S(1)} custom-call(f32[128,128]{1,0:T(8,128)S(1)} %cholesky.197), custom_call_target="Cholesky" | custom-call | tf_op jit(solution)/shard_map/jit(cholesky)/cholesky | solution.py:82
  454.1 0.6 compare_reduce_fusion.1
  454.8 9.8 %custom-call.15 = f32[1,128,128]{1,2,0:T(8,128)S(1)} custom-call(f32[1,128,128]{2,1,0:T(8,128)S(1)} %get-tuple-element.47), custom_call_target="InvertDiagBlocksLowerTriangular" | custom-call | tf_op jit(solution)/shard_map/jit(cholesky)/cholesky | solution.py:82
  464.8 0.3 convolution_subtract_fusion.5
  465.1 11.8 %cholesky.181 = f32[128,128]{1,0:T(8,128)S(1)} custom-call(f32[128,128]{1,0:T(8,128)S(1)} %convolution_subtract_fusion.5), custom_call_target="Cholesky" | custom-call | tf_op jit(solution)/shard_map/jit(cholesky)/cholesky | solution.py:82
  476.9 0.6 compare_reduce_fusion
  478.9 4.0 while.5
  479.0 0.6 fusion.62
  479.5 1.4 bitcast_dynamic-update-slice_fusion.5
  481.0 0.6 fusion.62
  481.5 1.4 bitcast_dynamic-update-slice_fusion.5
  482.9 19.7 %custom-call.16 = f32[2,128,128]{1,2,0:T(8,128)S(1)} custom-call(f32[2,128,128]{2,1,0:T(8,128)S(1)} %get-tuple-element.21), custom_call_target="InvertDiagBlocksLowerTriangular" | custom-call | tf_op jit(solution)/shard_map/triangular_solve/custom-call.0 | solution.py:84
  502.6 0.3 fusion.14
  502.9 0.3 convolution_subtract_fusion.3
  503.2 0.3 fusion.21
  503.5 1.3 convolution_subtract_fusion.2
  504.8 0.4 convolution_select_fusion
  505.3 4.3 stack.8
  509.6 6.6 all-to-all-start.5
  516.8 0.8 pad_maximum_fusion.1
  517.7 182.7 %all-to-all-done.5 = f32[32,128,512]{2,1,0:T(8,128)} async-done(((f32[32,128,512]{2,1,0:T(8,128)}), f32[32,128,512]{2,1,0:T(8,128)}, u32[]{:S(2)}, u32[]{:S(2)}) %all-to-all-start.5) | async-done | bytes 8388640 | tf_op jit(solution)/shard_map/all_to_all | solution.py:143
  700.3 2.4 convolution_subtract_fusion.1
  (49 shorter events, 2.1 us)
Async XLA Ops:
  7.2 99.1 %all-gather.3.cloned.1.call-start = ((), (), s32[]{:S(2)}) async-start(), calls=%async_computation.6 | async-start | bytes 8650752 | tf_op jit(solution)/shard_map/all_gather | solution.py:119
  114.8 9.6 %copy-start.1 = (f32[512,128]{1,0:T(8,128)S(1)}, f32[512,128]{1,0:T(8,128)}, u32[]{:S(2)}) copy-start(f32[512,128]{1,0:T(8,128)} %param.5) | copy-start | bytes 786436
  114.8 72.2 %all-to-all-start = ((f32[16,128,256]{2,1,0:T(8,128)}), f32[16,128,256]{2,1,0:T(8,128)S(1)}, u32[]{:S(2)}, u32[]{:S(2)}) async-start(f32[16,128,256]{2,1,0:T(8,128)} %bitcast.101), calls=%async_computation | async-start | bytes 4194304 | tf_op jit(solution)/shard_map/all_to_all | solution.py:26
  124.3 153.9 %all-gather.5.cloned.1.call-start = ((), (), s32[]{:S(2)}) async-start(), calls=%async_computation.7 | async-start | bytes 2228224 | tf_op jit(solution)/shard_map/all_gather | solution.py:15
  302.5 17.6 %all-to-all-start.2 = ((f32[32,8,256]{2,1,0:T(8,128)}), f32[32,8,256]{2,1,0:T(8,128)S(1)}, u32[]{:S(2)}, u32[]{:S(2)}) async-start(f32[32,8,256]{2,1,0:T(8,128)} %broadcast_in_dim.4), calls=%async_computation.2 | async-start | bytes 524288 | tf_op jit(solution)/shard_map/all_to_all | solution.py:43
  417.9 22.3 %all-to-all-start.4 = ((f32[32,1,4096]{2,1,0:T(1,128)}), f32[32,1,4096]{2,1,0:T(1,128)S(1)}, u32[]{:S(2)}, u32[]{:S(2)}) async-start(f32[32,1,4096]{2,1,0:T(1,128)} %broadcast_in_dim.5), calls=%async_computation.4 | async-start | bytes 1048576 | tf_op jit(solution)/shard_map/all_to_all | solution.py:43
  505.3 195.1 %copy-start = (f32[128,512]{1,0:T(8,128)}, f32[128,512]{1,0:T(8,128)S(1)}, u32[]{:S(2)}) copy-start(f32[128,512]{1,0:T(8,128)S(1)} %pad_maximum_fusion.4) | copy-start | bytes 786436
  509.6 190.8 %all-to-all-start.5 = ((f32[32,128,512]{2,1,0:T(8,128)}), f32[32,128,512]{2,1,0:T(8,128)}, u32[]{:S(2)}, u32[]{:S(2)}) async-start(f32[32,128,512]{2,1,0:T(8,128)} %stack.8), calls=%async_computation.5 | async-start | bytes 16777216 | tf_op jit(solution)/shard_map/all_to_all | solution.py:143
Sparse Core Ops, SparseCore 0:
  10.0 96.2 all-gather.2
  188.0 90.1 all-gather.4
